TPU v7x, 32 devices: a whole 2x2x4 slice. The times are simulated.
32 devices in a mesh: row: 4 (over x, core), col: 8 (over z, y).
Axes of the slice: x: 2, y: 2, z: 4, core: 2. Of those that a mesh axis runs over, the one named last changes fastest.
Arguments:
- matrix: float32 [2048, 8192], P('col', 'row'), may hold values from -6 to 6
- basis: float32 [8192, 512], P(('row', 'col')), may hold values from -0.0625 to 0.0625
Outputs:
- root: float32 [512, 512], P('row', 'col')
- right: float32 [2048, 512], P('col')
All inputs are finite; a program needn't handle non-finite values.
Results may differ from a plain program's by a relative error of at most 0.00018.
Values sent between devices are 32-bit elements; how exact they have to be, the bound alone decides.
A program may use at most 64 MiB of HBM per device.

v0:
```python
import jax
import jax.numpy as jnp
from jax import lax
from jax.sharding import PartitionSpec as P

ITERS = 8


def polar_steps(gram, width):
    highest = lax.Precision.HIGHEST
    scale = jnp.sqrt(jnp.sum(gram * gram) + 1e-06)
    ident = jnp.eye(width, dtype=jnp.float32)
    upper = gram / scale
    lower = ident
    for step in range(ITERS):
        middle = 0.5 * (3.0 * ident - jnp.dot(lower, upper, precision=highest))
        upper = jnp.dot(upper, middle, precision=highest)
        lower = jnp.dot(middle, lower, precision=highest)
    return (upper, lower, jnp.sqrt(scale))


def local(matrix, basis):
    highest = lax.Precision.HIGHEST
    width = basis.shape[1]
    nrow = lax.axis_size("row")
    ncol = lax.axis_size("col")
    partial_proj = lax.dot_general(
        lax.all_gather(basis, "col", axis=0, tiled=True),
        matrix,
        (((0,), (1,)), ((), ())),
        precision=highest,
    )
    proj = lax.psum(partial_proj, "row")
    gram = lax.psum(jnp.dot(proj, proj.T, precision=highest), "col")
    upper, lower, root_scale = polar_steps(gram, width)
    right = jnp.dot(proj.T, lower, precision=highest) / root_scale
    root_full = upper * root_scale
    row_len = width // nrow
    col_len = width // ncol
    root = lax.dynamic_slice(
        root_full,
        (lax.axis_index("row") * row_len, lax.axis_index("col") * col_len),
        (row_len, col_len),
    )
    return (root, right)


def solution(mesh):
    return jax.shard_map(
        local,
        mesh=mesh,
        in_specs=(P("col", "row"), P(("row", "col"), None)),
        out_specs=(P("row", "col"), P("col", None)),
        check_vma=False,
    )
```

profile of v0, /device:TPU:0, one launch (start us, length us, event | category | flops | bytes accessed | tf_op | source)
XLA Modules:
  0.0 268.9 jit_solution(109907291531495080)
XLA Ops:
  7.2 0.0 copy-start
  7.2 0.0 all-gather.2.cloned.1.call-start
  7.2 0.7 all-gather.2.cloned.1.call-update
  7.9 0.0 all-reduce.3.cloned.1.call-start
  8.0 77.7 %all-gather.2.cloned.1.call-done = f32[2048,512]{1,0:T(8,128)} async-done(((f32[256,512]{1,0:T(8,128)}), f32[2048,512]{1,0:T(8,128)}) %all-gather.2.cloned.1.call-update) | async-done | bytes 4194320 | tf_op jit(solution)/shard_map/all_gather | solution.py:28
  85.7 0.0 copy-done
  85.7 9.6 %fusion.10 = f32[512,256]{1,0:T(8,128)} fusion(f32[2048,512]{1,0:T(8,128)} %all-gather.2.cloned.1.call-done, f32[256,2048]{1,0:T(8,128)S(1)} %copy-done), kind=kOutput, calls=%fused_computation.23 | convolution fusion | flops 3221225472 | bytes 6815744 | tf_op jit(solution)/shard_map/dot_general | solution.py:27
  95.3 0.0 all-reduce.3.cloned.1.call-update
  95.3 0.2 all-reduce.5.cloned.1.call-start
  95.5 31.9 %all-reduce.3.cloned.1.call-done = f32[512,256]{1,0:T(8,128)} async-done(((f32[512,256]{1,0:T(8,128)}), f32[512,256]{1,0:T(8,128)}) %all-reduce.3.cloned.1.call-update) | async-done | bytes 524304 | tf_op jit(solution)/shard_map/psum | solution.py:33
  127.4 3.2 %fusion.11 = f32[512,512]{1,0:T(8,128)} fusion(f32[512,256]{1,0:T(8,128)} %all-reduce.3.cloned.1.call-done), kind=kOutput, calls=%fused_computation.24 | convolution fusion | flops 805306368 | bytes 1572864 | tf_op jit(solution)/shard_map/dot_general | solution.py:34
  130.6 0.0 all-reduce.5.cloned.1.call-update
  130.7 78.7 %all-reduce.5.cloned.1.call-done = f32[512,512]{1,0:T(8,128)} async-done(((f32[512,512]{1,0:T(8,128)}), f32[512,512]{1,0:T(8,128)}) %all-reduce.5.cloned.1.call-update) | async-done | bytes 1048592 | tf_op jit(solution)/shard_map/psum | solution.py:34
  209.4 0.0 copy-start.3
  209.4 2.2 multiply_reduce_fusion
  212.3 2.3 fusion.7
  214.6 1.0 fusion.8
  215.6 0.0 copy-done.3
  215.6 1.9 fusion.9
  217.5 1.9 fusion
  219.3 1.8 fusion.12
  221.2 1.8 fusion.13
  223.0 2.1 fusion.1
  225.1 1.8 fusion.15
  227.0 1.8 fusion.14
  228.8 1.8 fusion.2
  230.7 1.8 fusion.17
  232.5 1.8 fusion.16
  234.4 1.9 fusion.3
  236.2 2.3 fusion.19
  238.5 1.8 fusion.18
  240.4 1.8 fusion.4
  242.2 1.8 fusion.21
  244.1 1.8 fusion.20
  245.9 1.8 fusion.5
  247.8 1.8 fusion.23
  249.7 3.0 %fusion.22 = f32[512,512]{1,0:T(8,128)} fusion(f32[512,512]{1,0:T(8,128)S(1)} %fusion.20, f32[512,512]{1,0:T(8,128)S(1)} %fusion.5), kind=kOutput, calls=%fused_computation.35 | convolution fusion | flops 1610612736 | bytes 3145728 | tf_op jit(solution)/shard_map/dot_general | solution.py:17
  252.7 0.0 copy-start.1
  252.7 0.0 copy-start.2
  252.7 3.2 %fusion.6 = f32[512,512]{1,0:T(8,128)S(1)} fusion(f32[512,512]{1,0:T(8,128)S(1)} %fusion.23, f32[512,512]{1,0:T(8,128)} %fusion.22), kind=kOutput, calls=%fused_computation.14 | convolution fusion | flops 1611661312 | bytes 3145728 | tf_op jit(solution)/shard_map/dot_general | solution.py:16
  255.9 1.8 fusion.25
  257.8 0.0 copy-done.1
  257.8 1.9 fusion.24
  259.7 0.6 dynamic-slice_multiply_fusion
  260.3 0.0 copy-done.2
  260.3 1.9 convolution_divide_fusion
Async XLA Ops:
  7.2 78.5 %copy-start = (f32[256,2048]{1,0:T(8,128)S(1)}, f32[256,2048]{1,0:T(8,128)}, u32[]{:S(2)}) copy-start(f32[256,2048]{1,0:T(8,128)} %param.2) | copy-start | bytes 6291460
  7.2 78.5 %all-gather.2.cloned.1.call-start = ((), (), s32[]{:S(2)}) async-start(), calls=%async_computation | async-start | bytes 4718592 | tf_op jit(solution)/shard_map/all_gather | solution.py:28
  7.9 119.5 %all-reduce.3.cloned.1.call-start = ((), (), s32[]{:S(2)}) async-start(), calls=%async_computation.1 | async-start | bytes 1048576 | tf_op jit(solution)/shard_map/psum | solution.py:33
  95.3 114.0 %all-reduce.5.cloned.1.call-start = ((), (), s32[]{:S(2)}) async-start(), calls=%async_computation.2 | async-start | bytes 2097152 | tf_op jit(solution)/shard_map/psum | solution.py:34
  209.4 6.2 %copy-start.3 = (f32[512,512]{1,0:T(8,128)S(1)}, f32[512,512]{1,0:T(8,128)}, u32[]{:S(2)}) copy-start(f32[512,512]{1,0:T(8,128)} %all-reduce.5.cloned.1.call-done) | copy-start | bytes 3145732
  252.7 5.1 %copy-start.1 = (f32[512,512]{1,0:T(8,128)S(1)}, f32[512,512]{1,0:T(8,128)}, u32[]{:S(2)}) copy-start(f32[512,512]{1,0:T(8,128)} %fusion.22) | copy-start | bytes 3145732
  252.7 7.6 %copy-start.2 = (f32[512,256]{1,0:T(8,128)S(1)}, f32[512,256]{1,0:T(8,128)}, u32[]{:S(2)}) copy-start(f32[512,256]{1,0:T(8,128)} %all-reduce.3.cloned.1.call-done) | copy-start | bytes 1572868
Sparse Core Ops, SparseCore 0:
  10.1 75.5 all-gather.1
  95.4 31.9 all-reduce.2
  130.9 78.3 all-reduce.4
where the time goes:
time: 274 us; the launch traced here: 269 us
  waiting for transfers between devices  189 us (69%)
  matrix products  61.9 us (23%)
  between operations  14.9 us (5%)
  other arithmetic  2.82 us (1%)
    psum x1, waiting for transfers between devices, local(): gram = lax.psum(jnp.dot(proj, proj.T, precision=highest), 'col')  78.7 us
    all_gather x1, waiting for transfers between devices, local(): lax.all_gather(basis, 'col', axis=0, tiled=True)  77.7 us
    psum x1, waiting for transfers between devices, local(): proj = lax.psum(partial_proj, 'row')  31.9 us
    dot_general x8, matrix products, polar_steps(): middle = 0.5 * (3.0 * ident - jnp.dot(lower, upper, precision=highest))  16.8 us
    dot_general x8, matrix products, polar_steps(): upper = jnp.dot(upper, middle, precision=highest)  16 us
    dot_general x8, matrix products, polar_steps(): lower = jnp.dot(middle, lower, precision=highest)  14.3 us
    dot_general x1, matrix products, local(): lax.dot_general(lax.all_gather(basis, 'col', axis=0, tiled=True), matrix,...  9.64 us
  transfers between devices with their start and end apart: 3, of which 3 were waited for; matrix products, arithmetic and copies ran while one was open for 0% of the time, Pallas kernels for 0%

commit v1 on v0

--- a/solution.py
+++ b/solution.py
@@ -30,7 +30,9 @@
         (((0,), (1,)), ((), ())),
         precision=highest,
     )
-    proj = lax.psum(partial_proj, "row")
+    proj = partial_proj
+    for hop in (1, 2):
+        proj = proj + lax.ppermute(proj, "row", [(dev, dev ^ hop) for dev in range(4)])
     gram = lax.psum(jnp.dot(proj, proj.T, precision=highest), "col")
     upper, lower, root_scale = polar_steps(gram, width)
     right = jnp.dot(proj.T, lower, precision=highest) / root_scale

time: 274 us -> 254 us (0.927)
  waiting for transfers between devices: 189 us -> 170 us
    psum x1 -> x0, waiting for transfers between devices: 31.9 us -> none  [local(): proj = lax.psum(partial_proj, 'row')]
    ppermute x0 -> x2, waiting for transfers between devices: none -> 14.4 us  [local(): lax.ppermute(proj, 'row', [(dev, dev ^ hop) for dev in range(4)])]
  transfers between devices with their start and end apart: 3 -> 4, of which waited for: 3 -> 4; matrix products, arithmetic and copies ran while one was open for 0% -> 0% of each run, Pallas kernels for 0% -> 0%
where the time goes in v1:
time: 254 us; the launch traced here: 251 us
  waiting for transfers between devices  170 us (67%)
  matrix products  60 us (24%)
  between operations  15.3 us (6%)
  other arithmetic  2.94 us (1%)
    all_gather x1, waiting for transfers between devices, local(): lax.all_gather(basis, 'col', axis=0, tiled=True)  77.7 us
    psum x1, waiting for transfers between devices, local(): gram = lax.psum(jnp.dot(proj, proj.T, precision=highest), 'col')  77 us
    dot_general x8, matrix products, polar_steps(): middle = 0.5 * (3.0 * ident - jnp.dot(lower, upper, precision=highest))  16.8 us
    dot_general x8, matrix products, polar_steps(): upper = jnp.dot(upper, middle, precision=highest)  16.1 us
    ppermute x2, waiting for transfers between devices, local(): lax.ppermute(proj, 'row', [(dev, dev ^ hop) for dev in range(4)])  14.4 us
    dot_general x8, matrix products, polar_steps(): lower = jnp.dot(middle, lower, precision=highest)  14.1 us
    dot_general x1, matrix products, local(): lax.dot_general(lax.all_gather(basis, 'col', axis=0, tiled=True), matrix,...  9.07 us
  transfers between devices with their start and end apart: 4, of which 4 were waited for; matrix products, arithmetic and copies ran while one was open for 0% of the time, Pallas kernels for 0%

profile of v1, /device:TPU:0, one launch (start us, length us, event | category | flops | bytes accessed | tf_op | source)
XLA Modules:
  0.0 250.5 jit_solution(4577243097004862450)
XLA Ops:
  7.2 0.0 copy-start
  7.2 0.0 all-gather.2.cloned.1.call-start
  7.2 0.7 all-gather.2.cloned.1.call-update
  7.9 0.0 all-reduce.2.cloned.1.call-start
  8.0 77.7 %all-gather.2.cloned.1.call-done = f32[2048,512]{1,0:T(8,128)} async-done(((f32[256,512]{1,0:T(8,128)}), f32[2048,512]{1,0:T(8,128)}) %all-gather.2.cloned.1.call-update) | async-done | bytes 4194320 | tf_op jit(solution)/shard_map/all_gather | solution.py:28
  85.7 0.0 copy-done
  85.7 9.1 %fusion.10 = f32[512,256]{1,0:T(8,128)S(1)} fusion(f32[2048,512]{1,0:T(8,128)} %all-gather.2.cloned.1.call-done, f32[256,2048]{1,0:T(8,128)S(1)} %copy-done), kind=kOutput, calls=%fused_computation.23 | convolution fusion | flops 3221225472 | bytes 6815744 | tf_op jit(solution)/shard_map/dot_general | solution.py:27
  94.7 0.1 collective-permute-start
  94.8 1.9 collective-permute-done
  96.7 0.1 add.17
  96.8 1.5 collective-permute-start.1
  98.3 12.5 %collective-permute-done.1 = f32[512,256]{1,0:T(8,128)S(1)} collective-permute-done((f32[512,256]{1,0:T(8,128)S(1)}, f32[512,256]{1,0:T(8,128)S(1)}, u32[]{:S(2)}, u32[]{:S(2)}) %collective-permute-start.1) | collective-permute-done | bytes 524320 | tf_op jit(solution)/shard_map/ppermute | solution.py:35
  110.8 0.1 add.18
  110.9 0.0 copy-start.2
  110.9 0.8 copy-done.2
  111.7 2.1 fusion.11
  113.8 0.0 all-reduce.2.cloned.1.call-update
  113.8 77.0 %all-reduce.2.cloned.1.call-done = f32[512,512]{1,0:T(8,128)} async-done(((f32[512,512]{1,0:T(8,128)}), f32[512,512]{1,0:T(8,128)}) %all-reduce.2.cloned.1.call-update) | async-done | bytes 1048592 | tf_op jit(solution)/shard_map/psum | solution.py:36
  190.8 0.0 copy-start.4
  190.8 2.2 multiply_reduce_fusion
  193.7 2.3 fusion.7
  196.0 1.0 fusion.8
  197.0 0.0 copy-done.4
  197.0 1.9 fusion.9
  198.9 1.8 fusion
  200.7 1.8 fusion.13
  202.6 1.8 fusion.12
  204.4 2.0 fusion.1
  206.5 1.8 fusion.15
  208.3 1.8 fusion.14
  210.2 1.9 fusion.2
  212.1 1.8 fusion.17
  213.9 1.8 fusion.16
  215.8 1.8 fusion.3
  217.6 2.1 fusion.19
  219.7 1.8 fusion.18
  221.6 1.9 fusion.4
  223.4 1.8 fusion.21
  225.3 1.8 fusion.20
  227.1 1.8 fusion.5
  229.0 1.8 fusion.23
  230.8 3.1 %fusion.22 = f32[512,512]{1,0:T(8,128)} fusion(f32[512,512]{1,0:T(8,128)S(1)} %fusion.20, f32[512,512]{1,0:T(8,128)S(1)} %fusion.5), kind=kOutput, calls=%fused_computation.35 | convolution fusion | flops 1610612736 | bytes 3145728 | tf_op jit(solution)/shard_map/dot_general | solution.py:17
  234.0 0.0 copy-start.1
  234.0 0.0 copy-start.3
  234.0 3.2 %fusion.6 = f32[512,512]{1,0:T(8,128)S(1)} fusion(f32[512,512]{1,0:T(8,128)S(1)} %fusion.23, f32[512,512]{1,0:T(8,128)} %fusion.22), kind=kOutput, calls=%fused_computation.14 | convolution fusion | flops 1611661312 | bytes 3145728 | tf_op jit(solution)/shard_map/dot_general | solution.py:16
  237.2 1.8 fusion.25
  239.0 0.0 copy-done.1
  239.1 1.9 fusion.24
  240.9 0.0 copy-done.3
  241.0 1.9 convolution_divide_fusion
  242.8 0.6 dynamic-slice_multiply_fusion
Async XLA Ops:
  7.2 78.5 %copy-start = (f32[256,2048]{1,0:T(8,128)S(1)}, f32[256,2048]{1,0:T(8,128)}, u32[]{:S(2)}) copy-start(f32[256,2048]{1,0:T(8,128)} %param.2) | copy-start | bytes 6291460
  7.2 78.5 %all-gather.2.cloned.1.call-start = ((), (), s32[]{:S(2)}) async-start(), calls=%async_computation | async-start | bytes 4718592 | tf_op jit(solution)/shard_map/all_gather | solution.py:28
  7.9 182.9 %all-reduce.2.cloned.1.call-start = ((), (), s32[]{:S(2)}) async-start(), calls=%async_computation.1 | async-start | bytes 2097152 | tf_op jit(solution)/shard_map/psum | solution.py:36
  94.7 2.0 collective-permute-start
  96.8 14.0 %collective-permute-start.1 = (f32[512,256]{1,0:T(8,128)S(1)}, f32[512,256]{1,0:T(8,128)S(1)}, u32[]{:S(2)}, u32[]{:S(2)}) collective-permute-start(f32[512,256]{1,0:T(8,128)S(1)} %add.17), channel_id=1, source_target_pairs={{0,16},{8,24},{16,0},{24,8},{1,17},{9,25},{17,1},{25,9},{2,18},{10... | collective-permute-start | bytes 1572872 | tf_op jit(solution)/shard_map/ppermute | solution.py:35
  110.9 0.8 copy-start.2
  190.8 6.2 %copy-start.4 = (f32[512,512]{1,0:T(8,128)S(1)}, f32[512,512]{1,0:T(8,128)}, u32[]{:S(2)}) copy-start(f32[512,512]{1,0:T(8,128)} %all-reduce.2.cloned.1.call-done) | copy-start | bytes 3145732
  234.0 5.1 %copy-start.1 = (f32[512,512]{1,0:T(8,128)S(1)}, f32[512,512]{1,0:T(8,128)}, u32[]{:S(2)}) copy-start(f32[512,512]{1,0:T(8,128)} %fusion.22) | copy-start | bytes 3145732
  234.0 7.0 %copy-start.3 = (f32[512,256]{1,0:T(8,128)S(1)}, f32[512,256]{1,0:T(8,128)}, u32[]{:S(2)}) copy-start(f32[512,256]{1,0:T(8,128)} %copy-done.2) | copy-start | bytes 1572868
Sparse Core Ops, SparseCore 0:
  10.1 75.5 all-gather.1
  113.9 76.8 all-reduce.1

commit v2 on v0

--- a/solution.py
+++ b/solution.py
@@ -25,7 +25,9 @@
     nrow = lax.axis_size("row")
     ncol = lax.axis_size("col")
     partial_proj = lax.dot_general(
-        lax.all_gather(basis, "col", axis=0, tiled=True),
+        jnp.concatenate(
+            lax.all_to_all(jnp.stack([basis] * lax.axis_size("col")), "col", 0, 0), axis=0
+        ),
         matrix,
         (((0,), (1,)), ((), ())),
         precision=highest,

time: 274 us -> 297 us (1.084)
  blocking collectives: 0 us -> 100 us
  waiting for transfers between devices: 189 us -> 111 us
    all_to_all x0 -> x1, blocking collectives: none -> 100 us  [local(): lax.all_to_all(jnp.stack([basis] * lax.axis_size('col')), 'col', 0, 0)]
    all_gather x1 -> x0, waiting for transfers between devices: 77.7 us -> none  [local(): lax.all_gather(basis, 'col', axis=0, tiled=True)]
  transfers between devices with their start and end apart: 3 -> 2, of which waited for: 3 -> 2; matrix products, arithmetic and copies ran while one was open for 0% -> 0% of each run, Pallas kernels for 0% -> 0%
where the time goes in v2:
time: 297 us; the launch traced here: 291 us
  waiting for transfers between devices  111 us (37%)
  blocking collectives  100 us (34%)
  matrix products  59.9 us (20%)
  between operations  15.2 us (5%)
    all_to_all x1, blocking collectives, local(): lax.all_to_all(jnp.stack([basis] * lax.axis_size('col')), 'col', 0, 0)  100 us
    psum x1, waiting for transfers between devices, local(): gram = lax.psum(jnp.dot(proj, proj.T, precision=highest), 'col')  78.7 us
    psum x1, waiting for transfers between devices, local(): proj = lax.psum(partial_proj, 'row')  32.4 us
    dot_general x8, matrix products, polar_steps(): middle = 0.5 * (3.0 * ident - jnp.dot(lower, upper, precision=highest))  16.8 us
    dot_general x8, matrix products, polar_steps(): upper = jnp.dot(upper, middle, precision=highest)  16 us
    dot_general x8, matrix products, polar_steps(): lower = jnp.dot(middle, lower, precision=highest)  14.3 us
    dot_general x1, matrix products, local(): lax.dot_general(jnp.concatenate(lax.all_to_all(jnp.stack([basis] * lax.ax...  7.59 us
  transfers between devices with their start and end apart: 2, of which 2 were waited for; matrix products, arithmetic and copies ran while one was open for 0% of the time, Pallas kernels for 0%

profile of v2, /device:TPU:0, one launch (start us, length us, event | category | flops | bytes accessed | tf_op | source)
XLA Modules:
  0.0 291.3 jit_solution(18194980883053425524)
XLA Ops:
  7.2 0.0 copy-start
  7.2 0.0 all-reduce.3.cloned.1.call-start
  7.2 1.7 stack.2
  8.9 100.3 %all_to_all.5 = f32[8,256,512]{2,1,0:T(8,128)S(1)} all-to-all(f32[8,256,512]{2,1,0:T(8,128)S(1)} %stack.2), channel_id=1, replica_groups=mesh['row'=4,'col'=8] {'col'}, dimensions={0} | all-to-all | bytes 8388608 | tf_op jit(solution)/shard_map/all_to_all | solution.py:29
  109.2 0.0 copy-done
  109.2 7.6 %fusion.10 = f32[512,256]{1,0:T(8,128)} fusion(f32[2048,512]{1,0:T(8,128)S(1)} %bitcast.51, f32[256,2048]{1,0:T(8,128)S(1)} %copy-done), kind=kOutput, calls=%fused_computation.23 | convolution fusion | flops 3221225472 | bytes 6815744 | tf_op jit(solution)/shard_map/dot_general | solution.py:27
  116.8 0.0 all-reduce.3.cloned.1.call-update
  116.8 0.2 all-reduce.5.cloned.1.call-start
  117.1 32.4 %all-reduce.3.cloned.1.call-done = f32[512,256]{1,0:T(8,128)} async-done(((f32[512,256]{1,0:T(8,128)}), f32[512,256]{1,0:T(8,128)}) %all-reduce.3.cloned.1.call-update) | async-done | bytes 524304 | tf_op jit(solution)/shard_map/psum | solution.py:35
  149.4 3.3 %fusion.11 = f32[512,512]{1,0:T(8,128)} fusion(f32[512,256]{1,0:T(8,128)} %all-reduce.3.cloned.1.call-done), kind=kOutput, calls=%fused_computation.24 | convolution fusion | flops 805306368 | bytes 1572864 | tf_op jit(solution)/shard_map/dot_general | solution.py:36
  152.7 0.0 all-reduce.5.cloned.1.call-update
  152.7 78.7 %all-reduce.5.cloned.1.call-done = f32[512,512]{1,0:T(8,128)} async-done(((f32[512,512]{1,0:T(8,128)}), f32[512,512]{1,0:T(8,128)}) %all-reduce.5.cloned.1.call-update) | async-done | bytes 1048592 | tf_op jit(solution)/shard_map/psum | solution.py:36
  231.4 0.0 copy-start.3
  231.4 2.2 multiply_reduce_fusion
  234.3 2.3 fusion.7
  236.6 1.0 fusion.8
  237.6 0.0 copy-done.3
  237.6 1.9 fusion.9
  239.5 1.9 fusion
  241.4 1.8 fusion.12
  243.2 1.8 fusion.13
  245.1 2.1 fusion.1
  247.2 1.8 fusion.15
  249.0 1.8 fusion.14
  250.9 1.8 fusion.2
  252.7 1.8 fusion.17
  254.6 1.8 fusion.16
  256.4 1.9 fusion.3
  258.3 2.3 fusion.19
  260.6 1.8 fusion.18
  262.4 1.8 fusion.4
  264.3 1.8 fusion.21
  266.2 1.8 fusion.20
  268.0 1.8 fusion.5
  269.9 1.8 fusion.23
  271.7 3.0 %fusion.22 = f32[512,512]{1,0:T(8,128)} fusion(f32[512,512]{1,0:T(8,128)S(1)} %fusion.20, f32[512,512]{1,0:T(8,128)S(1)} %fusion.5), kind=kOutput, calls=%fused_computation.35 | convolution fusion | flops 1610612736 | bytes 3145728 | tf_op jit(solution)/shard_map/dot_general | solution.py:17
  274.8 0.0 copy-start.1
  274.8 0.0 copy-start.2
  274.8 3.2 %fusion.6 = f32[512,512]{1,0:T(8,128)S(1)} fusion(f32[512,512]{1,0:T(8,128)S(1)} %fusion.23, f32[512,512]{1,0:T(8,128)} %fusion.22), kind=kOutput, calls=%fused_computation.14 | convolution fusion | flops 1611661312 | bytes 3145728 | tf_op jit(solution)/shard_map/dot_general | solution.py:16
  278.0 1.8 fusion.25
  279.8 0.0 copy-done.1
  279.9 1.9 fusion.24
  281.7 0.6 dynamic-slice_multiply_fusion
  282.4 0.0 copy-done.2
  282.4 1.9 convolution_divide_fusion
Async XLA Ops:
  7.2 102.1 %copy-start = (f32[256,2048]{1,0:T(8,128)S(1)}, f32[256,2048]{1,0:T(8,128)}, u32[]{:S(2)}) copy-start(f32[256,2048]{1,0:T(8,128)} %param.2) | copy-start | bytes 6291460
  7.2 142.2 %all-reduce.3.cloned.1.call-start = ((), (), s32[]{:S(2)}) async-start(), calls=%async_computation.1 | async-start | bytes 1048576 | tf_op jit(solution)/shard_map/psum | solution.py:35
  116.8 114.6 %all-reduce.5.cloned.1.call-start = ((), (), s32[]{:S(2)}) async-start(), calls=%async_computation.2 | async-start | bytes 2097152 | tf_op jit(solution)/shard_map/psum | solution.py:36
  231.4 6.2 %copy-start.3 = (f32[512,512]{1,0:T(8,128)S(1)}, f32[512,512]{1,0:T(8,128)}, u32[]{:S(2)}) copy-start(f32[512,512]{1,0:T(8,128)} %all-reduce.5.cloned.1.call-done) | copy-start | bytes 3145732
  274.8 5.1 %copy-start.1 = (f32[512,512]{1,0:T(8,128)S(1)}, f32[512,512]{1,0:T(8,128)}, u32[]{:S(2)}) copy-start(f32[512,512]{1,0:T(8,128)} %fusion.22) | copy-start | bytes 3145732
  274.8 7.6 %copy-start.2 = (f32[512,256]{1,0:T(8,128)S(1)}, f32[512,256]{1,0:T(8,128)}, u32[]{:S(2)}) copy-start(f32[512,256]{1,0:T(8,128)} %all-reduce.3.cloned.1.call-done) | copy-start | bytes 1572868
Sparse Core Ops, SparseCore 0:
  117.0 32.4 all-reduce.2
  152.9 78.4 all-reduce.4
